TPU v7x, 32 devices: a whole 2x2x4 slice. The times are simulated.
32 devices in a mesh: dp: 16 (over z, y, core), fsdp: 2 (over x).
Axes of the slice: x: 2, y: 2, z: 4, core: 2. Of those that a mesh axis runs over, the one named last changes fastest.
Arguments:
- patches: bfloat16 [16384, 768], P(('dp', 'fsdp')), may hold values from -6 to 6
- cotangent: bfloat16 [16384, 768], P(('dp', 'fsdp')), may hold values from -6 to 6
- lengths: int32 [32, 4], P(('dp', 'fsdp')), may hold values from 0 to 512, as said below
- arrange: int32 [16384], P(('dp', 'fsdp')), may hold values from 0 to 511, as said below
- first_gain: bfloat16 [768], P('dp'), may hold values from 0.3984375 to 1.59375
- first_shift: bfloat16 [768], P('dp'), may hold values from -1.5 to 1.5
- project_weight: bfloat16 [768, 2304], P('dp', 'fsdp'), may hold values from -0.21875 to 0.21875
- query_bias: bfloat16 [768], P('dp'), may hold values from -1.5 to 1.5
- value_bias: bfloat16 [768], P('dp'), may hold values from -1.5 to 1.5
- output_weight: bfloat16 [768, 768], P('dp', 'fsdp'), may hold values from -1.75 to 1.75
- output_bias: bfloat16 [768], P('dp'), may hold values from -1.5 to 1.5
- second_gain: bfloat16 [768], P('dp'), may hold values from 0.3984375 to 1.59375
- second_shift: bfloat16 [768], P('dp'), may hold values from -1.5 to 1.5
- up_weight: bfloat16 [768, 3072], P('dp', 'fsdp'), may hold values from -0.21875 to 0.21875
- up_bias: bfloat16 [3072], P('dp'), may hold values from -1.5 to 1.5
- down_weight: bfloat16 [3072, 768], P('dp', 'fsdp'), may hold values from -0.109375 to 0.109375
- down_bias: bfloat16 [768], P('dp'), may hold values from -1.5 to 1.5
Outputs:
- encoded: bfloat16 [16384, 768], P(('dp', 'fsdp'))
- grad_patches: bfloat16 [16384, 768], P(('dp', 'fsdp'))
- grad_first_gain: float32 [768], P('dp')
- grad_first_shift: float32 [768], P('dp')
- grad_project_weight: float32 [768, 2304], P('dp', 'fsdp')
- grad_query_bias: float32 [768], P('dp')
- grad_value_bias: float32 [768], P('dp')
- grad_output_weight: float32 [768, 768], P('dp', 'fsdp')
- grad_output_bias: float32 [768], P('dp')
- grad_second_gain: float32 [768], P('dp')
- grad_second_shift: float32 [768], P('dp')
- grad_up_weight: float32 [768, 3072], P('dp', 'fsdp')
- grad_up_bias: float32 [3072], P('dp')
- grad_down_weight: float32 [3072, 768], P('dp', 'fsdp')
- grad_down_bias: float32 [768], P('dp')
Inputs may be any that keep to these rules, and one draw needn't show every extreme that they name: Each block's 4 lengths sum to at least 384 and at most 512; slots may be empty; in every draw some block holds a single sequence of 512 rows. `arrange`: each block's 512 entries are a permutation of 0 to 511.
All inputs are finite; a program needn't handle non-finite values.
Results may differ from a plain program's by a relative error of at most 0.012.
Values may be sent and summed in bfloat16 or wider, within the bound.
A program may use at most 128 MiB of HBM per device.

v0:
```python
import jax
import jax.numpy as jnp
from jax import lax
from jax.sharding import PartitionSpec as P

HEADS = 12
HEAD = 64
NORM_EPSILON = 1e-12
MASK_VALUE = -1e30
ROOT_HALF = 0.7071067811865476


def norm_rows(values, norm_gain, norm_shift):
    center = values - jnp.mean(values, axis=-1, keepdims=True)
    spread = jnp.mean(center * center, axis=-1, keepdims=True)
    return center * lax.rsqrt(spread + NORM_EPSILON) * norm_gain + norm_shift


def gelu_exact(values):
    return 0.5 * values * (1.0 + lax.erf(values * ROOT_HALF))


def slot_labels(lengths, arrange):
    total_rows = arrange.shape[0]
    slot_ends = jnp.cumsum(lengths[0])
    position = jnp.arange(total_rows, dtype=jnp.int32)
    slot_index = jnp.sum((position[:, None] >= slot_ends[None, :]).astype(jnp.int32), axis=1)
    return jnp.zeros((total_rows,), jnp.int32).at[arrange].set(slot_index)


def matmul(left_side, right_side, pattern):
    return jnp.einsum(pattern, left_side, right_side, preferred_element_type=jnp.float32)


def column_sums(values):
    return jnp.sum(values.astype(jnp.float32), axis=0)


def local(
    patches,
    cotangent,
    lengths,
    arrange,
    first_gain,
    first_shift,
    project_weight,
    query_bias,
    value_bias,
    output_weight,
    output_bias,
    second_gain,
    second_shift,
    up_weight,
    up_bias,
    down_weight,
    down_bias,
):
    arrived, cot_rows = (
        lax.all_to_all(patches, "dp", split_axis=0, concat_axis=0, tiled=True),
        lax.all_to_all(cotangent, "dp", split_axis=0, concat_axis=0, tiled=True),
    )
    total_rows, width = patches.shape
    labels = slot_labels(lengths, arrange)
    live_rows = (labels < lengths.shape[1]).astype(jnp.float32)[:, None]
    project_part, output_part, up_part, down_part = (
        lax.all_gather(project_weight, "fsdp", axis=1, tiled=True),
        lax.all_gather(output_weight, "fsdp", axis=1, tiled=True),
        lax.all_gather(up_weight, "fsdp", axis=1, tiled=True),
        lax.all_gather(down_weight, "fsdp", axis=1, tiled=True),
    )
    attn_set = (
        lax.all_gather(first_gain, "dp", axis=0, tiled=True),
        lax.all_gather(first_shift, "dp", axis=0, tiled=True),
        lax.all_gather(project_part, "dp", axis=0, tiled=True),
        lax.all_gather(query_bias, "dp", axis=0, tiled=True),
        lax.all_gather(value_bias, "dp", axis=0, tiled=True),
        lax.all_gather(output_part, "dp", axis=0, tiled=True),
        lax.all_gather(output_bias, "dp", axis=0, tiled=True),
    )
    inputs = arrived.astype(jnp.float32)
    gain_one = attn_set[0].astype(jnp.float32)
    shift_one = attn_set[1].astype(jnp.float32)
    normed_one = norm_rows(inputs, gain_one, shift_one)
    normed_low = normed_one.astype(jnp.bfloat16)
    joint = jnp.dot(normed_low, attn_set[2], preferred_element_type=jnp.float32)
    queries = (
        (joint[:, :width] + attn_set[3].astype(jnp.float32))
        .astype(jnp.bfloat16)
        .reshape(total_rows, HEADS, HEAD)
    )
    key_rows = joint[:, width : 2 * width].astype(jnp.bfloat16).reshape(total_rows, HEADS, HEAD)
    value_rows = (
        (joint[:, 2 * width :] + attn_set[4].astype(jnp.float32))
        .astype(jnp.bfloat16)
        .reshape(total_rows, HEADS, HEAD)
    )
    score_scale = HEAD ** (-0.5)
    block_rows = min(512, total_rows)
    block_starts = jnp.arange(total_rows // block_rows, dtype=jnp.int32) * block_rows

    def block_scores():
        raw_scores = matmul(queries, key_rows, "qhe,khe->hqk") * score_scale
        visible = labels[:, None] == labels[None, :]
        return (queries, jnp.where(visible[None], raw_scores, MASK_VALUE))

    def attend(start):
        query_block, scores = block_scores()
        top_score = jnp.max(scores, axis=-1, keepdims=True)
        weights = jnp.exp(scores - top_score)
        totals = jnp.sum(weights, axis=-1, keepdims=True)
        prob_low = (weights / totals).astype(jnp.bfloat16)
        mixed_rows = matmul(prob_low, value_rows, "hqk,khe->qhe")
        return (mixed_rows.astype(jnp.bfloat16), (top_score + jnp.log(totals))[:, :, 0])

    mixed_blocks, log_totals = lax.map(attend, block_starts)
    attended = mixed_blocks.reshape(total_rows, width)
    attn_out = jnp.dot(attended, attn_set[5], preferred_element_type=jnp.float32) + attn_set[
        6
    ].astype(jnp.float32)
    hidden = inputs + attn_out
    mlp_set = (
        lax.all_gather(second_gain, "dp", axis=0, tiled=True),
        lax.all_gather(second_shift, "dp", axis=0, tiled=True),
        lax.all_gather(up_part, "dp", axis=0, tiled=True),
        lax.all_gather(up_bias, "dp", axis=0, tiled=True),
        lax.all_gather(down_part, "dp", axis=0, tiled=True),
        lax.all_gather(down_bias, "dp", axis=0, tiled=True),
    )
    gain_two = mlp_set[0].astype(jnp.float32)
    shift_two = mlp_set[1].astype(jnp.float32)
    normed_two = norm_rows(hidden, gain_two, shift_two)
    normed_two_low = normed_two.astype(jnp.bfloat16)
    pre_act = jnp.dot(normed_two_low, mlp_set[2], preferred_element_type=jnp.float32) + mlp_set[
        3
    ].astype(jnp.float32)
    activated = gelu_exact(pre_act).astype(jnp.bfloat16)
    branch = jnp.dot(activated, mlp_set[4], preferred_element_type=jnp.float32) + mlp_set[5].astype(
        jnp.float32
    )
    encoded_rows = live_rows * (hidden + branch)
    grad_out = live_rows * cot_rows.astype(jnp.float32)
    grad_branch = grad_out.astype(jnp.bfloat16)
    again_two = (
        lax.all_gather(second_gain, "dp", axis=0, tiled=True),
        lax.all_gather(second_shift, "dp", axis=0, tiled=True),
        lax.all_gather(up_part, "dp", axis=0, tiled=True),
        lax.all_gather(up_bias, "dp", axis=0, tiled=True),
        lax.all_gather(down_part, "dp", axis=0, tiled=True),
        lax.all_gather(down_bias, "dp", axis=0, tiled=True),
    )
    grad_down = matmul(activated, grad_branch, "tf,td->fd")
    grad_downbias = column_sums(grad_branch)
    grad_activ = matmul(grad_branch, again_two[4], "td,fd->tf")
    grad_pre = jax.vjp(gelu_exact, pre_act)[1](grad_activ)[0].astype(jnp.bfloat16)
    grad_up = matmul(normed_two_low, grad_pre, "td,tf->df")
    grad_upbias = column_sums(grad_pre)
    grad_normed_two = matmul(grad_pre, again_two[2], "tf,df->td")
    norm_pull_two = jax.vjp(
        norm_rows, hidden, again_two[0].astype(jnp.float32), again_two[1].astype(jnp.float32)
    )[1]
    grad_hidden_part, grad_gain_two, grad_shift_two = norm_pull_two(grad_normed_two)
    grad_hidden = grad_out + grad_hidden_part
    mlp_sums = (
        lax.psum_scatter(grad_up, "dp", scatter_dimension=0, tiled=True),
        lax.psum_scatter(grad_down, "dp", scatter_dimension=0, tiled=True),
        lax.psum_scatter(grad_gain_two, "dp", scatter_dimension=0, tiled=True),
        lax.psum_scatter(grad_shift_two, "dp", scatter_dimension=0, tiled=True),
        lax.psum_scatter(grad_upbias, "dp", scatter_dimension=0, tiled=True),
        lax.psum_scatter(grad_downbias, "dp", scatter_dimension=0, tiled=True),
    )
    again_one = (
        lax.all_gather(first_gain, "dp", axis=0, tiled=True),
        lax.all_gather(first_shift, "dp", axis=0, tiled=True),
        lax.all_gather(project_part, "dp", axis=0, tiled=True),
        lax.all_gather(query_bias, "dp", axis=0, tiled=True),
        lax.all_gather(value_bias, "dp", axis=0, tiled=True),
        lax.all_gather(output_part, "dp", axis=0, tiled=True),
        lax.all_gather(output_bias, "dp", axis=0, tiled=True),
    )
    grad_attn = grad_hidden.astype(jnp.bfloat16)
    grad_output = matmul(attended, grad_attn, "td,te->de")
    grad_outbias = column_sums(grad_attn)
    grad_attended = (
        matmul(grad_attn, again_one[5], "te,de->td")
        .astype(jnp.bfloat16)
        .reshape(total_rows, HEADS, HEAD)
    )

    def back_block(carry, block_item):
        key_acc, value_acc = carry
        start, log_block = block_item
        query_block, scores = block_scores()
        prob_full = jnp.exp(scores - log_block[:, :, None])
        prob_low = prob_full.astype(jnp.bfloat16)
        value_acc = value_acc + matmul(prob_low, grad_attended, "hqk,qhe->khe")
        grad_prob = matmul(grad_attended, value_rows, "qhe,khe->hqk")
        inner = jnp.sum(prob_full * grad_prob, axis=-1, keepdims=True)
        grad_scores = (prob_full * (grad_prob - inner)).astype(jnp.bfloat16)
        query_grad = matmul(grad_scores, key_rows, "hqk,khe->qhe") * score_scale
        key_acc = key_acc + matmul(grad_scores, query_block, "hqk,qhe->khe") * score_scale
        return ((key_acc, value_acc), query_grad.astype(jnp.bfloat16))

    zero_acc = jnp.zeros((total_rows, HEADS, HEAD), jnp.float32)
    (key_grad_sum, value_grad_sum), query_grads = lax.scan(
        back_block, (zero_acc, zero_acc), (block_starts, log_totals)
    )
    grad_queries = query_grads.reshape(total_rows, width)
    grad_keys = key_grad_sum.reshape(total_rows, width).astype(jnp.bfloat16)
    grad_values = value_grad_sum.reshape(total_rows, width).astype(jnp.bfloat16)
    grad_joint = jnp.concatenate([grad_queries, grad_keys, grad_values], axis=1)
    grad_project = matmul(normed_low, grad_joint, "td,tf->df")
    grad_querybias = column_sums(grad_queries)
    grad_valuebias = column_sums(grad_values)
    grad_normed_one = matmul(grad_joint, again_one[2], "tf,df->td")
    norm_pull_one = jax.vjp(
        norm_rows, inputs, again_one[0].astype(jnp.float32), again_one[1].astype(jnp.float32)
    )[1]
    grad_input_part, grad_gain_one, grad_shift_one = norm_pull_one(grad_normed_one)
    grad_inputs = grad_hidden + grad_input_part
    attn_sums = (
        lax.psum_scatter(grad_project, "dp", scatter_dimension=0, tiled=True),
        lax.psum_scatter(grad_output, "dp", scatter_dimension=0, tiled=True),
        lax.psum_scatter(grad_gain_one, "dp", scatter_dimension=0, tiled=True),
        lax.psum_scatter(grad_shift_one, "dp", scatter_dimension=0, tiled=True),
        lax.psum_scatter(grad_querybias, "dp", scatter_dimension=0, tiled=True),
        lax.psum_scatter(grad_valuebias, "dp", scatter_dimension=0, tiled=True),
        lax.psum_scatter(grad_outbias, "dp", scatter_dimension=0, tiled=True),
    )
    matrix_parts = (
        lax.psum_scatter(
            attn_sums[0].astype(jnp.bfloat16), "fsdp", scatter_dimension=1, tiled=True
        ).astype(jnp.float32),
        lax.psum_scatter(
            attn_sums[1].astype(jnp.bfloat16), "fsdp", scatter_dimension=1, tiled=True
        ).astype(jnp.float32),
        lax.psum_scatter(
            mlp_sums[0].astype(jnp.bfloat16), "fsdp", scatter_dimension=1, tiled=True
        ).astype(jnp.float32),
        lax.psum_scatter(
            mlp_sums[1].astype(jnp.bfloat16), "fsdp", scatter_dimension=1, tiled=True
        ).astype(jnp.float32),
    )
    vector_parts = lax.psum(
        (
            attn_sums[2],
            attn_sums[3],
            attn_sums[4],
            attn_sums[5],
            attn_sums[6],
            mlp_sums[2],
            mlp_sums[3],
            mlp_sums[4],
            mlp_sums[5],
        ),
        "fsdp",
    )
    encoded_back, grad_back = (
        lax.all_to_all(
            encoded_rows.astype(jnp.bfloat16), "dp", split_axis=0, concat_axis=0, tiled=True
        ),
        lax.all_to_all(
            grad_inputs.astype(jnp.bfloat16), "dp", split_axis=0, concat_axis=0, tiled=True
        ),
    )
    return (
        encoded_back,
        grad_back,
        vector_parts[0],
        vector_parts[1],
        matrix_parts[0],
        vector_parts[2],
        vector_parts[3],
        matrix_parts[1],
        vector_parts[4],
        vector_parts[5],
        vector_parts[6],
        matrix_parts[2],
        vector_parts[7],
        matrix_parts[3],
        vector_parts[8],
    )


def solution(mesh):
    return jax.shard_map(
        local,
        mesh=mesh,
        in_specs=(
            P(("dp", "fsdp"), None),
            P(("dp", "fsdp"), None),
            P(("dp", "fsdp"), None),
            P(("dp", "fsdp")),
            P("dp"),
            P("dp"),
            P("dp", "fsdp"),
            P("dp"),
            P("dp"),
            P("dp", "fsdp"),
            P("dp"),
            P("dp"),
            P("dp"),
            P("dp", "fsdp"),
            P("dp"),
            P("dp", "fsdp"),
            P("dp"),
        ),
        out_specs=(
            P(("dp", "fsdp"), None),
            P(("dp", "fsdp"), None),
            P("dp"),
            P("dp"),
            P("dp", "fsdp"),
            P("dp"),
            P("dp"),
            P("dp", "fsdp"),
            P("dp"),
            P("dp"),
            P("dp"),
            P("dp", "fsdp"),
            P("dp"),
            P("dp", "fsdp"),
            P("dp"),
        ),
        check_vma=False,
    )
```

profile of v0, /device:TPU:0, one launch (start us, length us, event | category | flops | bytes accessed | tf_op | source)
XLA Modules:
  0.0 716.2 jit_solution(9440607187867650082)
XLA Ops:
  7.2 8.7 %all_gather.59 = bf16[48,2304]{1,0:T(8,128)(2,1)} all-gather(bf16[48,1152]{1,0:T(8,128)(2,1)} %param.23), channel_id=1, replica_groups=mesh['dp'=16,'fsdp'=2] {'fsdp'}, dimensions={1}, use_global_device_ids=true | all-gather | bytes 331776 | tf_op jit(solution)/shard_map/all_gather | solution.py:66
  16.0 4.9 all_gather.63
  21.1 7.0 all_gather.68
  28.2 6.0 all-to-all-start
  34.2 6.9 all_gather.71
  41.4 14.7 %all-to-all-done = bf16[16,32,768]{2,1,0:T(8,128)(2,1)S(1)} async-done(((bf16[16,32,768]{2,1,0:T(8,128)(2,1)}), bf16[16,32,768]{2,1,0:T(8,128)(2,1)S(1)}, u32[]{:S(2)}, u32[]{:S(2)}) %all-to-all-start) | async-done | bytes 786464 | tf_op jit(solution)/shard_map/all_to_all | solution.py:59
  56.1 14.3 %all-to-all-start.2 = ((bf16[16,32,768]{2,1,0:T(8,128)(2,1)}), bf16[16,32,768]{2,1,0:T(8,128)(2,1)S(1)}, u32[]{:S(2)}, u32[]{:S(2)}) async-start(bf16[16,32,768]{2,1,0:T(8,128)(2,1)} %bitcast.13), calls=%async_computation.2 | async-start | bytes 1572864 | tf_op jit(solution)/shard_map/all_to_all | solution.py:60
  74.6 66.2 %all-reduce.20 = (bf16[768]{0:T(1024)(128)(2,1)S(1)}, bf16[768]{0:T(1024)(128)(2,1)S(1)}, bf16[768]{0:T(1024)(128)(2,1)S(1)}, bf16[768]{0:T(1024)(128)(2,1)S(1)}...) all-reduce(bf16[768]{0:T(1024)(128)(2,1)S(1)} %dynamic-update-slice, ...), channel_id=1, replica_groups=mesh['dp'=16,'fsdp'=2] {'dp'}, use_global_device_ids=true, to_apply=%add.1 | all-reduce | flops 9216 | bytes 36864
  164.5 4.5 fusion.24
  171.8 7.2 %fusion.39 = f32[512,3072]{1,0:T(8,128)} fusion(bf16[768,3072]{1,0:T(8,128)(2,1)} %all-gather.9.cloned.1.call-done, f32[512,768]{1,0:T(8,128)S(1)} %get-tuple-element.114, f32[768]{0:T(1024)} %convert_element_type.197, f32[768]{0:T(1024)S(1)} %convert_element_type.196, f32[512]{0:T(512)S(1)} %fusion.28, f32[512]{0:T(512)S(1)} %broadcast_multiply_fusion.1), kind=kOutput, calls=%fused_computation.87 | convolution fusion | flops 2417885184 | bytes 12593152 | tf_op jit(solution)/shard_map/dot_general | solution.py:133
  179.0 41.7 %all-gather.11.cloned.1.call-done = bf16[3072,768]{1,0:T(8,128)(2,1)} async-done(((bf16[192,768]{1,0:T(8,128)(2,1)}), bf16[3072,768]{1,0:T(8,128)(2,1)}) %all-gather.11.cloned.1.call-update) | async-done | bytes 4718608 | tf_op jit(solution)/shard_map/all_gather | solution.py:126
  220.7 9.5 %convert_reduce_fusion = (f32[3072]{0:T(1024)S(1)}, bf16[512,3072]{1,0:T(8,128)(2,1)S(1)}, bf16[512,3072]{1,0:T(8,128)(2,1)}) fusion(f32[512,3072]{1,0:T(8,128)} %fusion.39, f32[3072]{0:T(1024)S(1)} %convert_element_type.199, bf16[512,768]{1,0:T(8,128)(2,1)} %fusion.20, bf16[3072,768]{1,0:T(8,128)(2,1)} %all-gather.11.cloned.1.call-done), kind=kOutput, calls=%fused_computation.10 | convolution fusion | flops 2444227584 | bytes 18112512 | tf_op jit(solution)/shard_map/td,fd->tf/dot_general | solution.py:32
  244.6 13.7 %multiply_reduce_fusion = (f32[12,512]{1,0:T(8,128)S(1)}, f32[12,512,512]{1,2,0:T(8,128)}) fusion(f32[12,512]{1,0:T(8,128)S(1)} %log_add_fusion, f32[12,512,512]{1,2,0:T(8,128)} %copy-done, pred[512,512]{0,1:T(8,128)(4,1)S(1)} %broadcast_compare_fusion, bf16[512,12,64]{0,2,1:T(8,128)(2,1)} %bitcast.111, bf16[512,12,64]{0,2,1:T(8,128)(2,1)} %bitcast.109), kind=kOutput, calls=%fused_computation.2 | convolution fusion | flops 418375680 | bytes 27049984 | tf_op jit(solution)/shard_map/while/body/eval_jaxpr/qhe,khe->hqk/dot_general | solution.py:32
  258.4 7.2 %multiply_convert_fusion = bf16[12,512,512]{1,2,0:T(8,128)(2,1)S(1)} fusion(f32[12,512,512]{1,2,0:T(8,128)} %get-tuple-element.117, f32[12,512]{1,0:T(8,128)S(1)} %get-tuple-element.116, f32[12,512]{1,0:T(8,128)S(1)} %log_add_fusion, f32[12,512,512]{1,2,0:T(8,128)S(1)} %bitcast.104, pred[512,512]{0,1:T(8,128)(4,1)S(1)} %broadcast_compare_fusion), kind=kLoop, calls=%fused_computation.1 | loop fusion | flops 18874368 | bytes 31768576 | tf_op jit(solution)/shard_map/while/body/eval_jaxpr/convert_element_type | solution.py:198
  274.0 4.9 fusion.25
  279.3 8.4 %fusion.47 = f32[3072,768]{1,0:T(8,128)} fusion(bf16[512,3072]{1,0:T(8,128)(2,1)} %get-tuple-element.106, bf16[512,768]{1,0:T(8,128)(2,1)} %fusion.20), kind=kOutput, calls=%fused_computation.94 | convolution fusion | flops 2415919104 | bytes 13369344 | tf_op jit(solution)/shard_map/tf,td->fd/dot_general | solution.py:32
  288.4 8.9 %fusion.38 = f32[768,3072]{1,0:T(8,128)} fusion(bf16[512,3072]{1,0:T(8,128)(2,1)} %copy-done.32, f32[512,768]{1,0:T(8,128)} %copy-done.5, f32[768]{0:T(1024)S(1)} %copy-done.16, f32[768]{0:T(1024)S(1)} %convert_element_type.196, f32[512]{0:T(512)S(1)} %fusion.28, f32[512]{0:T(512)S(1)} %broadcast_multiply_fusion.1), kind=kOutput, calls=%fused_computation.86 | convolution fusion | flops 2417885184 | bytes 14166016 | tf_op jit(solution)/shard_map/td,tf->df/dot_general | solution.py:32
  298.0 7.2 %multiply_convert_fusion.5 = bf16[512,768]{1,0:T(8,128)(2,1)} fusion(f32[512,768]{1,0:T(8,128)} %copy-done.5, bf16[512,3072]{1,0:T(8,128)(2,1)} %get-tuple-element.106, bf16[3072,768]{1,0:T(8,128)(2,1)} %all-gather.11.cloned.1.call-done, f32[768]{0:T(1024)S(1)} %convert_element_type.201, f32[512]{0:T(512)S(1)} %compare_convert_fusion), kind=kOutput, calls=%fused_computation.52 | convolution fusion | flops 2417491968 | bytes 10228736 | tf_op jit(solution)/shard_map/dot_general | solution.py:137
  309.5 5.0 fusion.40
  318.5 80.6 %reduce-scatter.15.cloned.1.call-done = f32[48,2304]{1,0:T(8,128)} async-done(((f32[768,2304]{1,0:T(8,128)}), f32[48,2304]{1,0:T(8,128)}) %reduce-scatter.15.cloned.1.call-update) | async-done | bytes 442384 | tf_op jit(solution)/shard_map/reduce_scatter | solution.py:221
  408.4 105.7 %reduce-scatter.23.cloned.1.call-done = f32[192,768]{1,0:T(8,128)} async-done(((f32[3072,768]{1,0:T(8,128)}), f32[192,768]{1,0:T(8,128)}) %reduce-scatter.23.cloned.1.call-update) | async-done | bytes 589840 | tf_op jit(solution)/shard_map/reduce_scatter | solution.py:165
  516.1 112.9 %reduce-scatter.19.cloned.1.call-done = f32[48,3072]{1,0:T(8,128)} async-done(((f32[768,3072]{1,0:T(8,128)}), f32[48,3072]{1,0:T(8,128)}) %reduce-scatter.19.cloned.1.call-update) | async-done | bytes 589840 | tf_op jit(solution)/shard_map/reduce_scatter | solution.py:164
  632.6 60.3 %all-reduce.18 = (f32[768]{0:T(1024)S(1)}, f32[768]{0:T(1024)S(1)}, f32[768]{0:T(1024)S(1)}, f32[768]{0:T(1024)S(1)}, f32[768]{0:T(1024)S(1)}, /*index=5*/f32[76...) all-reduce(f32[768]{0:T(1024)S(1)} %get-tuple-element.68, ...), channel_id=2, replica_groups=mesh['dp'=16,'fsdp'=2] {'dp'}, use_global_device_ids=true, to_apply=%region_15.16.clone | all-reduce | flops 9216 | bytes 73728
  693.5 5.5 all-reduce.19
  (210 shorter events, 86.2 us)
Async XLA Ops:
  7.2 139.5 %all-gather.5.cloned.1.call-start = ((), (), s32[]{:S(2)}) async-start(), calls=%async_computation.12 | async-start | bytes 3760128 | tf_op jit(solution)/shard_map/all_gather | solution.py:74
  15.9 153.0 %all-gather.7.cloned.1.call-start = ((), (), s32[]{:S(2)}) async-start(), calls=%async_computation.13 | async-start | bytes 1253376 | tf_op jit(solution)/shard_map/all_gather | solution.py:77
  21.0 52.2 %copy-start.25 = (bf16[48]{0:T(256)(128)(2,1)S(1)}, bf16[48]{0:T(256)(128)(2,1)}, u32[]{:S(2)}) copy-start(bf16[48]{0:T(256)(128)(2,1)} %param.24) | copy-start | bytes 292
  21.0 52.4 %copy-start.26 = (bf16[48]{0:T(256)(128)(2,1)S(1)}, bf16[48]{0:T(256)(128)(2,1)}, u32[]{:S(2)}) copy-start(bf16[48]{0:T(256)(128)(2,1)} %param.25) | copy-start | bytes 292
  21.0 52.6 %copy-start.27 = (bf16[48]{0:T(256)(128)(2,1)S(1)}, bf16[48]{0:T(256)(128)(2,1)}, u32[]{:S(2)}) copy-start(bf16[48]{0:T(256)(128)(2,1)} %param.21) | copy-start | bytes 292
  21.0 52.8 %copy-start.28 = (bf16[48]{0:T(256)(128)(2,1)S(1)}, bf16[48]{0:T(256)(128)(2,1)}, u32[]{:S(2)}) copy-start(bf16[48]{0:T(256)(128)(2,1)} %param.22) | copy-start | bytes 292
  21.0 53.0 %copy-start.29 = (bf16[48]{0:T(256)(128)(2,1)S(1)}, bf16[48]{0:T(256)(128)(2,1)}, u32[]{:S(2)}) copy-start(bf16[48]{0:T(256)(128)(2,1)} %param.33) | copy-start | bytes 292
  21.0 53.3 %copy-start.30 = (bf16[192]{0:T(256)(128)(2,1)S(1)}, bf16[192]{0:T(256)(128)(2,1)}, u32[]{:S(2)}) copy-start(bf16[192]{0:T(256)(128)(2,1)} %param.31) | copy-start | bytes 1156
  21.1 120.3 %copy-start.19 = (s32[512]{0:T(512)S(1)}, s32[512]{0:T(512)}, u32[]{:S(2)}) copy-start(s32[512]{0:T(512)} %param.20) | copy-start | bytes 6148
  21.1 150.7 %all-gather.9.cloned.1.call-start = ((), (), s32[]{:S(2)}) async-start(), calls=%async_computation.14 | async-start | bytes 5013504 | tf_op jit(solution)/shard_map/all_gather | solution.py:124
  28.2 27.9 %all-to-all-start = ((bf16[16,32,768]{2,1,0:T(8,128)(2,1)}), bf16[16,32,768]{2,1,0:T(8,128)(2,1)S(1)}, u32[]{:S(2)}, u32[]{:S(2)}) async-start(bf16[16,32,768]{2,1,0:T(8,128)(2,1)} %bitcast.119), calls=%async_computation | async-start | bytes 1572864 | tf_op jit(solution)/shard_map/all_to_all | solution.py:59
  34.1 186.5 %all-gather.11.cloned.1.call-start = ((), (), s32[]{:S(2)}) async-start(), calls=%async_computation.15 | async-start | bytes 5013504 | tf_op jit(solution)/shard_map/all_gather | solution.py:126
  56.1 89.2 %all-to-all-start.2 = ((bf16[16,32,768]{2,1,0:T(8,128)(2,1)}), bf16[16,32,768]{2,1,0:T(8,128)(2,1)S(1)}, u32[]{:S(2)}, u32[]{:S(2)}) async-start(bf16[16,32,768]{2,1,0:T(8,128)(2,1)} %bitcast.13), calls=%async_computation.2 | async-start | bytes 1572864 | tf_op jit(solution)/shard_map/all_to_all | solution.py:60
  70.4 246.2 %reduce-scatter.17.cloned.1.call-start = ((), (), s32[]{:S(2)}) async-start(), calls=%async_computation.17 | async-start | bytes 2506752 | tf_op jit(solution)/shard_map/reduce_scatter | solution.py:222
  171.4 58.8 %copy-start.5 = (f32[512,768]{1,0:T(8,128)}, f32[512,768]{1,0:T(8,128)S(1)}, u32[]{:S(2)}) copy-start(f32[512,768]{1,0:T(8,128)S(1)} %get-tuple-element.114) | copy-start | bytes 4718596
  244.3 154.8 %reduce-scatter.15.cloned.1.call-start = ((), (), s32[]{:S(2)}) async-start(), calls=%async_computation.16 | async-start | bytes 7520256 | tf_op jit(solution)/shard_map/reduce_scatter | solution.py:221
  279.0 235.1 %reduce-scatter.23.cloned.1.call-start = ((), (), s32[]{:S(2)}) async-start(), calls=%async_computation.20 | async-start | bytes 10027008 | tf_op jit(solution)/shard_map/reduce_scatter | solution.py:165
  287.7 341.3 %reduce-scatter.19.cloned.1.call-start = ((), (), s32[]{:S(2)}) async-start(), calls=%async_computation.18 | async-start | bytes 10027008 | tf_op jit(solution)/shard_map/reduce_scatter | solution.py:164
  305.2 98.8 %all-to-all-start.1 = ((bf16[16,32,768]{2,1,0:T(8,128)(2,1)}), bf16[16,32,768]{2,1,0:T(8,128)(2,1)}, u32[]{:S(2)}, u32[]{:S(2)}) async-start(bf16[16,32,768]{2,1,0:T(8,128)(2,1)} %bitcast.120), calls=%async_computation.1 | async-start | bytes 1572864 | tf_op jit(solution)/shard_map/all_to_all | solution.py:258
  309.5 389.6 %reduce-scatter.27.cloned.1.call-start = ((), (), s32[]{:S(2)}) async-start(), calls=%async_computation.22 | async-start | bytes 294912
  318.4 382.3 %reduce-scatter.25.cloned.1.call-start = ((), (), s32[]{:S(2)}) async-start(), calls=%async_computation.21 | async-start | bytes 884736
  404.0 295.1 %all-to-all-start.3 = ((bf16[16,32,768]{2,1,0:T(8,128)(2,1)}), bf16[16,32,768]{2,1,0:T(8,128)(2,1)S(1)}, u32[]{:S(2)}, u32[]{:S(2)}) async-start(bf16[16,32,768]{2,1,0:T(8,128)(2,1)} %bitcast.114), calls=%async_computation.3 | async-start | bytes 1572864 | tf_op jit(solution)/shard_map/all_to_all | solution.py:261
  408.3 294.2 %reduce-scatter.29.cloned.1.call-start = ((), (), s32[]{:S(2)}) async-start(), calls=%async_computation.23 | async-start | bytes 589824
  516.1 188.3 %reduce-scatter.21.cloned.1.call-start = ((), (), s32[]{:S(2)}) async-start(), calls=%async_computation.19 | async-start | bytes 442368 | tf_op jit(solution)/shard_map/reduce_scatter | solution.py:236
  (28 other events, 373.1 us)
Sparse Core Ops, SparseCore 0:
  16.0 54.1 all-gather.4
  72.6 39.9 all-gather.6
  114.8 51.9 all-gather.8
  169.0 51.6 all-gather.10
  244.4 61.7 reduce-scatter.16
  310.1 88.9 reduce-scatter.14
  403.2 110.8 reduce-scatter.22
  518.1 110.8 reduce-scatter.18
  631.8 10.6 reduce-scatter.26
  644.7 15.3 reduce-scatter.24
  662.9 13.1 reduce-scatter.28
  678.8 12.0 reduce-scatter.20
where the time goes:
time: 722 us; the launch traced here: 716 us
  waiting for transfers between devices  356 us (49%)
  blocking collectives  160 us (22%)
  matrix products  94.2 us (13%)
  starting transfers between devices  29.8 us (4%)
  local copies, waits for them, and re-layouts  29.7 us (4%)
  other arithmetic  29.2 us (4%)
  between operations  17.9 us (2%)
    unnamed x2, blocking collectives  126 us
    reduce_scatter x1, waiting for transfers between devices, local(): lax.psum_scatter(grad_up, 'dp', scatter_dimension=0, tiled=True)  113 us
    reduce_scatter x1, waiting for transfers between devices, local(): lax.psum_scatter(grad_down, 'dp', scatter_dimension=0, tiled=True)  106 us
    reduce_scatter x1, waiting for transfers between devices, local(): lax.psum_scatter(grad_project, 'dp', scatter_dimension=0, tiled=True)  80.6 us
    dot_general x14, matrix products, matmul(): jnp.einsum(pattern, left_side, right_side, preferred_element_type=jnp.flo...  72.9 us
    all_gather x1, waiting for transfers between devices, local(): lax.all_gather(down_part, 'dp', axis=0, tiled=True)  41.7 us
    unnamed x108, local copies, waits for them, and re-layouts  18.6 us
    all_to_all x1, waiting for transfers between devices, local(): lax.all_to_all(patches, 'dp', split_axis=0, concat_axis=0, tiled=True)  14.7 us
  transfers between devices with their start and end apart: 16, of which 5 were waited for; matrix products, arithmetic and copies ran while one was open for 17% of the time, Pallas kernels for 0%

commit v1 on v0

--- a/solution.py
+++ b/solution.py
@@ -8,6 +8,21 @@
 NORM_EPSILON = 1e-12
 MASK_VALUE = -1e30
 ROOT_HALF = 0.7071067811865476
+
+
+def settle_the_ratios(u):
+    state_now = jax.lax.axis_index("dp")
+    even = jax.lax.axis_size("dp")
+    small, reply = (even, state_now)
+    h_now, mixed_arr = (u, 1)
+    while mixed_arr < small:
+        far_arr = tuple(((idx, idx ^ mixed_arr) for idx in range(small)))
+        arr_next = jax.lax.ppermute(h_now, axis_name="dp", perm=far_arr)
+        carry_in = jnp.concatenate([h_now, arr_next], axis=0)
+        new = jnp.concatenate([arr_next, h_now], axis=0)
+        h_now = jnp.where(reply & mixed_arr == 0, carry_in, new)
+        mixed_arr = 2 * mixed_arr
+    return h_now
 
 
 def norm_rows(values, norm_gain, norm_shift):
@@ -123,7 +138,7 @@
         lax.all_gather(second_shift, "dp", axis=0, tiled=True),
         lax.all_gather(up_part, "dp", axis=0, tiled=True),
         lax.all_gather(up_bias, "dp", axis=0, tiled=True),
-        lax.all_gather(down_part, "dp", axis=0, tiled=True),
+        settle_the_ratios(down_part),
         lax.all_gather(down_bias, "dp", axis=0, tiled=True),
     )
     gain_two = mlp_set[0].astype(jnp.float32)

time: 722 us -> 822 us (1.14)
  waiting for transfers between devices: 356 us -> 446 us
    ppermute x0 -> x4, waiting for transfers between devices: none -> 86.6 us  [settle_the_ratios(): arr_next = jax.lax.ppermute(h_now, axis_name='dp', perm=far_arr)]
    reduce_scatter x1, waiting for transfers between devices: 80.6 us -> 89.9 us  [local(): lax.psum_scatter(grad_project, 'dp', scatter_dimension=0, tiled=True)]
    select_n x0 -> x3, other arithmetic: none -> 8.96 us  [settle_the_ratios(): h_now = jnp.where(reply & mixed_arr == 0, carry_in, new)]
    unnamed x108 -> x118, local copies, waits for them, and re-layouts: 18.6 us -> 16.7 us
  transfers between devices with their start and end apart: 16 -> 20, of which waited for: 5 -> 9; matrix products, arithmetic and copies ran while one was open for 17% -> 16% of each run, Pallas kernels for 0% -> 0%
where the time goes in v1:
time: 822 us; the launch traced here: 817 us
  waiting for transfers between devices  446 us (54%)
  blocking collectives  159 us (19%)
  matrix products  94.6 us (12%)
  other arithmetic  37.1 us (5%)
  starting transfers between devices  33.8 us (4%)
  local copies, waits for them, and re-layouts  27.9 us (3%)
  between operations  17.7 us (2%)
    unnamed x2, blocking collectives  126 us
    reduce_scatter x1, waiting for transfers between devices, local(): lax.psum_scatter(grad_up, 'dp', scatter_dimension=0, tiled=True)  113 us
    reduce_scatter x1, waiting for transfers between devices, local(): lax.psum_scatter(grad_down, 'dp', scatter_dimension=0, tiled=True)  100 us
    reduce_scatter x1, waiting for transfers between devices, local(): lax.psum_scatter(grad_project, 'dp', scatter_dimension=0, tiled=True)  89.9 us
    ppermute x4, waiting for transfers between devices, settle_the_ratios(): arr_next = jax.lax.ppermute(h_now, axis_name='dp', perm=far_arr)  86.6 us
    dot_general x14, matrix products, matmul(): jnp.einsum(pattern, left_side, right_side, preferred_element_type=jnp.flo...  72.7 us
    all_gather x1, waiting for transfers between devices, local(): lax.all_gather(down_part, 'dp', axis=0, tiled=True)  41.4 us
    unnamed x118, local copies, waits for them, and re-layouts  16.7 us
  transfers between devices with their start and end apart: 20, of which 9 were waited for; matrix products, arithmetic and copies ran while one was open for 16% of the time, Pallas kernels for 0%

profile of v1, /device:TPU:0, one launch (start us, length us, event | category | flops | bytes accessed | tf_op | source)
XLA Modules:
  0.0 816.5 jit_solution(17445156893522034238)
XLA Ops:
  7.2 8.7 %all_gather.58 = bf16[48,2304]{1,0:T(8,128)(2,1)} all-gather(bf16[48,1152]{1,0:T(8,128)(2,1)} %param.23), channel_id=1, replica_groups=mesh['dp'=16,'fsdp'=2] {'fsdp'}, dimensions={1}, use_global_device_ids=true | all-gather | bytes 331776 | tf_op jit(solution)/shard_map/all_gather | solution.py:81
  21.1 7.0 all_gather.67
  28.2 6.0 all-to-all-start
  34.2 6.9 all_gather.70
  41.3 14.7 %all-to-all-done = bf16[16,32,768]{2,1,0:T(8,128)(2,1)S(1)} async-done(((bf16[16,32,768]{2,1,0:T(8,128)(2,1)}), bf16[16,32,768]{2,1,0:T(8,128)(2,1)S(1)}, u32[]{:S(2)}, u32[]{:S(2)}) %all-to-all-start) | async-done | bytes 786464 | tf_op jit(solution)/shard_map/all_to_all | solution.py:74
  56.1 14.5 %all-to-all-start.2 = ((bf16[16,32,768]{2,1,0:T(8,128)(2,1)}), bf16[16,32,768]{2,1,0:T(8,128)(2,1)S(1)}, u32[]{:S(2)}, u32[]{:S(2)}) async-start(bf16[16,32,768]{2,1,0:T(8,128)(2,1)} %bitcast.13), calls=%async_computation.2 | async-start | bytes 1572864 | tf_op jit(solution)/shard_map/all_to_all | solution.py:75
  74.8 66.1 %all-reduce.20 = (bf16[768]{0:T(1024)(128)(2,1)S(1)}, bf16[768]{0:T(1024)(128)(2,1)S(1)}, bf16[768]{0:T(1024)(128)(2,1)S(1)}, bf16[768]{0:T(1024)(128)(2,1)S(1)}...) all-reduce(bf16[768]{0:T(1024)(128)(2,1)S(1)} %dynamic-update-slice, ...), channel_id=1, replica_groups=mesh['dp'=16,'fsdp'=2] {'dp'}, use_global_device_ids=true, to_apply=%add.1 | all-reduce | flops 9216 | bytes 36864
  172.1 7.2 fusion.47
  179.3 41.4 %all-gather.11.cloned.1.call-done = bf16[3072,768]{1,0:T(8,128)(2,1)} async-done(((bf16[192,768]{1,0:T(8,128)(2,1)}), bf16[3072,768]{1,0:T(8,128)(2,1)}) %all-gather.11.cloned.1.call-update) | async-done | bytes 4718608 | tf_op jit(solution)/shard_map/all_gather | solution.py:163
  220.7 9.5 %convert_reduce_fusion = (f32[3072]{0:T(1024)S(1)}, bf16[512,3072]{1,0:T(8,128)(2,1)S(1)}, bf16[512,3072]{1,0:T(8,128)(2,1)}) fusion(f32[512,3072]{1,0:T(8,128)} %fusion.47, f32[3072]{0:T(1024)S(1)} %convert_element_type.199, bf16[512,768]{1,0:T(8,128)(2,1)} %fusion.27, bf16[3072,768]{1,0:T(8,128)(2,1)} %all-gather.11.cloned.1.call-done), kind=kOutput, calls=%fused_computation.10 | convolution fusion | flops 2444227584 | bytes 18112512 | tf_op jit(solution)/shard_map/td,fd->tf/dot_general | solution.py:47
  245.1 13.7 %multiply_reduce_fusion = (f32[12,512]{1,0:T(8,128)S(1)}, f32[12,512,512]{1,2,0:T(8,128)}) fusion(f32[12,512]{1,0:T(8,128)S(1)} %log_add_fusion, f32[12,512,512]{1,2,0:T(8,128)} %copy-done, pred[512,512]{0,1:T(8,128)(4,1)S(1)} %broadcast_compare_fusion, bf16[512,12,64]{0,2,1:T(8,128)(2,1)} %bitcast.109, bf16[512,12,64]{0,2,1:T(8,128)(2,1)} %bitcast.107), kind=kOutput, calls=%fused_computation.2 | convolution fusion | flops 418375680 | bytes 27049984 | tf_op jit(solution)/shard_map/while/body/eval_jaxpr/qhe,khe->hqk/dot_general | solution.py:47
  258.9 7.2 multiply_convert_fusion
  280.0 8.4 %fusion.55 = f32[3072,768]{1,0:T(8,128)} fusion(bf16[512,3072]{1,0:T(8,128)(2,1)} %get-tuple-element.106, bf16[512,768]{1,0:T(8,128)(2,1)} %fusion.27), kind=kOutput, calls=%fused_computation.106 | convolution fusion | flops 2415919104 | bytes 13369344 | tf_op jit(solution)/shard_map/tf,td->fd/dot_general | solution.py:47
  289.1 8.9 %fusion.46 = f32[768,3072]{1,0:T(8,128)} fusion(bf16[512,3072]{1,0:T(8,128)(2,1)} %copy-done.37, f32[512,768]{1,0:T(8,128)} %copy-done.5, f32[768]{0:T(1024)S(1)} %copy-done.19, f32[768]{0:T(1024)S(1)} %convert_element_type.196, f32[512]{0:T(512)S(1)} %fusion.35, f32[512]{0:T(512)S(1)} %broadcast_multiply_fusion.1), kind=kOutput, calls=%fused_computation.98 | convolution fusion | flops 2417885184 | bytes 14166016 | tf_op jit(solution)/shard_map/td,tf->df/dot_general | solution.py:47
  303.3 15.3 %collective-permute-done.1 = bf16[384,768]{1,0:T(8,128)(2,1)} collective-permute-done((bf16[384,768]{1,0:T(8,128)(2,1)}, bf16[384,768]{1,0:T(8,128)(2,1)}, u32[]{:S(2)}, u32[]{:S(2)}) %collective-permute-start.1) | collective-permute-done | bytes 589856 | tf_op jit(solution)/shard_map/ppermute | solution.py:20
  323.2 42.5 %collective-permute-done.2 = bf16[768,768]{1,0:T(8,128)(2,1)} collective-permute-done((bf16[768,768]{1,0:T(8,128)(2,1)}, bf16[768,768]{1,0:T(8,128)(2,1)}, u32[]{:S(2)}, u32[]{:S(2)}) %collective-permute-start.2) | collective-permute-done | bytes 1179680 | tf_op jit(solution)/shard_map/ppermute | solution.py:20
  382.9 89.9 %reduce-scatter.15.cloned.1.call-done = f32[48,2304]{1,0:T(8,128)} async-done(((f32[768,2304]{1,0:T(8,128)}), f32[48,2304]{1,0:T(8,128)}) %reduce-scatter.15.cloned.1.call-update) | async-done | bytes 442384 | tf_op jit(solution)/shard_map/reduce_scatter | solution.py:236
  474.9 27.4 %collective-permute-done.3 = bf16[1536,768]{1,0:T(8,128)(2,1)} collective-permute-done((bf16[1536,768]{1,0:T(8,128)(2,1)}, bf16[1536,768]{1,0:T(8,128)(2,1)}, u32[]{:S(2)}, u32[]{:S(2)}) %collective-permute-start.3) | collective-permute-done | bytes 2359328 | tf_op jit(solution)/shard_map/ppermute | solution.py:20
  502.3 7.9 multiply_convert_fusion.5
  510.2 5.3 all-to-all-start.1
  515.6 100.2 %reduce-scatter.23.cloned.1.call-done = f32[192,768]{1,0:T(8,128)} async-done(((f32[3072,768]{1,0:T(8,128)}), f32[192,768]{1,0:T(8,128)}) %reduce-scatter.23.cloned.1.call-update) | async-done | bytes 589840 | tf_op jit(solution)/shard_map/reduce_scatter | solution.py:180
  617.8 112.9 %reduce-scatter.19.cloned.1.call-done = f32[48,3072]{1,0:T(8,128)} async-done(((f32[768,3072]{1,0:T(8,128)}), f32[48,3072]{1,0:T(8,128)}) %reduce-scatter.19.cloned.1.call-update) | async-done | bytes 589840 | tf_op jit(solution)/shard_map/reduce_scatter | solution.py:179
  734.3 60.3 %all-reduce.18 = (f32[768]{0:T(1024)S(1)}, f32[768]{0:T(1024)S(1)}, f32[768]{0:T(1024)S(1)}, f32[768]{0:T(1024)S(1)}, f32[768]{0:T(1024)S(1)}, /*index=5*/f32[76...) all-reduce(f32[768]{0:T(1024)S(1)} %get-tuple-element.68, ...), channel_id=2, replica_groups=mesh['dp'=16,'fsdp'=2] {'dp'}, use_global_device_ids=true, to_apply=%region_15.16.clone | all-reduce | flops 9216 | bytes 73728
  795.3 5.5 all-reduce.19
  (231 shorter events, 111.4 us)
Async XLA Ops:
  7.2 139.8 %all-gather.5.cloned.1.call-start = ((), (), s32[]{:S(2)}) async-start(), calls=%async_computation.12 | async-start | bytes 3760128 | tf_op jit(solution)/shard_map/all_gather | solution.py:89
  15.9 153.3 %all-gather.7.cloned.1.call-start = ((), (), s32[]{:S(2)}) async-start(), calls=%async_computation.13 | async-start | bytes 1253376 | tf_op jit(solution)/shard_map/all_gather | solution.py:92
  21.1 120.4 %copy-start.23 = (s32[512]{0:T(512)S(1)}, s32[512]{0:T(512)}, u32[]{:S(2)}) copy-start(s32[512]{0:T(512)} %param.20) | copy-start | bytes 6148
  21.1 151.0 %all-gather.9.cloned.1.call-start = ((), (), s32[]{:S(2)}) async-start(), calls=%async_computation.14 | async-start | bytes 5013504 | tf_op jit(solution)/shard_map/all_gather | solution.py:139
  28.2 27.9 %all-to-all-start = ((bf16[16,32,768]{2,1,0:T(8,128)(2,1)}), bf16[16,32,768]{2,1,0:T(8,128)(2,1)S(1)}, u32[]{:S(2)}, u32[]{:S(2)}) async-start(bf16[16,32,768]{2,1,0:T(8,128)(2,1)} %bitcast.118), calls=%async_computation | async-start | bytes 1572864 | tf_op jit(solution)/shard_map/all_to_all | solution.py:74
  34.1 186.6 %all-gather.11.cloned.1.call-start = ((), (), s32[]{:S(2)}) async-start(), calls=%async_computation.15 | async-start | bytes 5013504 | tf_op jit(solution)/shard_map/all_gather | solution.py:163
  56.1 89.4 %all-to-all-start.2 = ((bf16[16,32,768]{2,1,0:T(8,128)(2,1)}), bf16[16,32,768]{2,1,0:T(8,128)(2,1)S(1)}, u32[]{:S(2)}, u32[]{:S(2)}) async-start(bf16[16,32,768]{2,1,0:T(8,128)(2,1)} %bitcast.13), calls=%async_computation.2 | async-start | bytes 1572864 | tf_op jit(solution)/shard_map/all_to_all | solution.py:75
  70.6 310.3 %reduce-scatter.17.cloned.1.call-start = ((), (), s32[]{:S(2)}) async-start(), calls=%async_computation.17 | async-start | bytes 2506752 | tf_op jit(solution)/shard_map/reduce_scatter | solution.py:237
  171.7 58.5 %copy-start.5 = (f32[512,768]{1,0:T(8,128)}, f32[512,768]{1,0:T(8,128)S(1)}, u32[]{:S(2)}) copy-start(f32[512,768]{1,0:T(8,128)S(1)} %get-tuple-element.114) | copy-start | bytes 4718596
  244.8 227.9 %reduce-scatter.15.cloned.1.call-start = ((), (), s32[]{:S(2)}) async-start(), calls=%async_computation.16 | async-start | bytes 7520256 | tf_op jit(solution)/shard_map/reduce_scatter | solution.py:236
  279.5 336.2 %reduce-scatter.23.cloned.1.call-start = ((), (), s32[]{:S(2)}) async-start(), calls=%async_computation.20 | async-start | bytes 10027008 | tf_op jit(solution)/shard_map/reduce_scatter | solution.py:180
  288.4 442.3 %reduce-scatter.19.cloned.1.call-start = ((), (), s32[]{:S(2)}) async-start(), calls=%async_computation.18 | async-start | bytes 10027008 | tf_op jit(solution)/shard_map/reduce_scatter | solution.py:179
  298.9 1.7 collective-permute-start
  302.8 15.8 %collective-permute-start.1 = (bf16[384,768]{1,0:T(8,128)(2,1)}, bf16[384,768]{1,0:T(8,128)(2,1)}, u32[]{:S(2)}, u32[]{:S(2)}) collective-permute-start(bf16[384,768]{1,0:T(8,128)(2,1)} %maximum_select_fusion.6), channel_id=1, source_target_pairs={{0,4},{2,6},{4,0},{6,2},{8,12},{10,14},{12,8},{14,10},{16,20},{18,... | collective-permute-start | bytes 1769480 | tf_op jit(solution)/shard_map/ppermute | solution.py:20
  321.7 44.0 %collective-permute-start.2 = (bf16[768,768]{1,0:T(8,128)(2,1)}, bf16[768,768]{1,0:T(8,128)(2,1)}, u32[]{:S(2)}, u32[]{:S(2)}) collective-permute-start(bf16[768,768]{1,0:T(8,128)(2,1)} %maximum_select_fusion.5), channel_id=1, source_target_pairs={{0,8},{2,10},{4,12},{6,14},{8,0},{10,2},{12,4},{14,6},{16,24},{18,... | collective-permute-start | bytes 3538952 | tf_op jit(solution)/shard_map/ppermute | solution.py:20
  369.5 132.8 %collective-permute-start.3 = (bf16[1536,768]{1,0:T(8,128)(2,1)}, bf16[1536,768]{1,0:T(8,128)(2,1)}, u32[]{:S(2)}, u32[]{:S(2)}) collective-permute-start(bf16[1536,768]{1,0:T(8,128)(2,1)} %maximum_select_fusion.2), channel_id=1, source_target_pairs={{0,16},{2,18},{4,20},{6,22},{8,24},{10,26},{12,28},{14,30},{16,0},... | collective-permute-start | bytes 7077896 | tf_op jit(solution)/shard_map/ppermute | solution.py:20
  376.4 125.9 %copy-start.6 = (f32[512,768]{1,0:T(8,128)S(1)}, f32[512,768]{1,0:T(8,128)}, u32[]{:S(2)}) copy-start(f32[512,768]{1,0:T(8,128)} %copy-done.5) | copy-start | bytes 4718596
  376.4 133.8 %all-to-all-start.3 = ((bf16[16,32,768]{2,1,0:T(8,128)(2,1)}), bf16[16,32,768]{2,1,0:T(8,128)(2,1)S(1)}, u32[]{:S(2)}, u32[]{:S(2)}) async-start(bf16[16,32,768]{2,1,0:T(8,128)(2,1)} %bitcast.113), calls=%async_computation.3 | async-start | bytes 1572864 | tf_op jit(solution)/shard_map/all_to_all | solution.py:276
  380.8 420.0 %reduce-scatter.27.cloned.1.call-start = ((), (), s32[]{:S(2)}) async-start(), calls=%async_computation.22 | async-start | bytes 294912
  382.7 419.8 %reduce-scatter.25.cloned.1.call-start = ((), (), s32[]{:S(2)}) async-start(), calls=%async_computation.21 | async-start | bytes 884736
  510.2 290.6 %all-to-all-start.1 = ((bf16[16,32,768]{2,1,0:T(8,128)(2,1)}), bf16[16,32,768]{2,1,0:T(8,128)(2,1)S(1)}, u32[]{:S(2)}, u32[]{:S(2)}) async-start(bf16[16,32,768]{2,1,0:T(8,128)(2,1)} %bitcast.119), calls=%async_computation.1 | async-start | bytes 1572864 | tf_op jit(solution)/shard_map/all_to_all | solution.py:273
  515.5 218.8 %copy-start.20 = (f32[768]{0:T(1024)S(1)}, f32[768]{0:T(1024)}, u32[]{:S(2)}) copy-start(f32[768]{0:T(1024)} %get-tuple-element.70) | copy-start | bytes 9220
  515.5 288.8 %reduce-scatter.29.cloned.1.call-start = ((), (), s32[]{:S(2)}) async-start(), calls=%async_computation.23 | async-start | bytes 589824
  617.8 188.3 %reduce-scatter.21.cloned.1.call-start = ((), (), s32[]{:S(2)}) async-start(), calls=%async_computation.19 | async-start | bytes 442368 | tf_op jit(solution)/shard_map/reduce_scatter | solution.py:251
  (37 other events, 840.8 us)
Sparse Core Ops, SparseCore 0:
  16.1 54.1 all-gather.4
  72.6 39.9 all-gather.6
  114.9 51.9 all-gather.8
  169.0 51.6 all-gather.10
  245.0 61.9 reduce-scatter.16
  310.9 161.8 reduce-scatter.14
  476.9 138.8 reduce-scatter.22
  619.8 110.8 reduce-scatter.18
  733.5 10.6 reduce-scatter.26
  746.4 15.3 reduce-scatter.24
  764.6 13.1 reduce-scatter.28
  780.5 12.1 reduce-scatter.20
